TPU v7x, 32 devices: a whole 2x2x4 slice. The times are simulated.
32 devices in a mesh: groups: 2 (over y), seq: 4 (over z), head: 4 (over x, core).
Axes of the slice: x: 2, y: 2, z: 4, core: 2. Of those that a mesh axis runs over, the one named last changes fastest.
Arguments:
- residual: bfloat16 [4096, 2560], P(('groups', 'seq'), 'head'), parts along dimension 0, may hold values from -6 to 6
- x_in: bfloat16 [4096, 5120], P(('groups', 'seq'), 'head'), parts along dimension 0, may hold values from -6 to 6
- bc_in: bfloat16 [4096, 256], P(('groups', 'seq')), parts along dimension 0, may hold values from -1.5 to 1.5
- z_in: bfloat16 [4096, 5120], P(('groups', 'seq'), 'head'), parts along dimension 0, may hold values from -6 to 6
- dt_raw: float32 [80, 4096], P('head', ('groups', 'seq')), parts along dimension 1, may hold values from -5 to 5
- dt_bias: float32 [80], P('head'), may hold values from -3 to 0
- decay_rate: float32 [80], P('head'), may hold values from 0.0003 to 0.15
- d_skip: float32 [80], P('head'), may hold values from 1 to 4
- conv_x_weight: bfloat16 [4, 5120], P(None, 'head'), may hold values from -3 to 3
- conv_x_bias: bfloat16 [5120], P('head'), may hold values from -3 to 3
- conv_bc_weight: bfloat16 [4, 256], replicated, may hold values from -3 to 3
- conv_bc_bias: bfloat16 [256], replicated, may hold values from -3 to 3
- norm_gain: bfloat16 [5120], P('head'), may hold values from 0.5 to 1.5
- out_weight: bfloat16 [5120, 2560], P('head'), may hold values from -0.078125 to 0.078125
- final_gain: bfloat16 [2560], replicated, may hold values from 0.5 to 1.5
- lm_weight: bfloat16 [2560, 25600], P('seq', 'head'), may hold values from -15.811388 to 15.811388
- targets: int32 [4096], P(('groups', 'seq')), parts along dimension 0, may hold values from 0 to 25599
- doc_lengths: int32 [8], P('groups'), parts along dimension 0, may hold values from 1 to 1536, as said below
Outputs:
- block_out: bfloat16 [4096, 2560], P(('groups', 'seq'), 'head'), parts along dimension 0
- doc_loss: float32 [8], P('groups'), parts along dimension 0
There are 2 independent parts, one for each index of `groups`. A program takes and returns all parts, laid end to end along the dimension named above; an argument that names none is the same for every part. Nothing has to cross between parts.
Inputs may be any that keep to these rules, and one draw needn't show every extreme that they name: `doc_lengths`: the lengths of a group's 4 documents, in the order in which they are packed into its 2048 tokens; they sum to 2048.
All inputs are finite; a program needn't handle non-finite values.
Results may differ from a plain program's by a relative error of at most 0.00145.
The roundings to bfloat16 on the way count: a program that leaves them out, or rounds other values in their place, can miss the bound.
Values may be sent and summed in bfloat16 or wider, within the bound.
A program may use at most 128 MiB of HBM per device.

v0:
```python
import functools

import jax
import jax.numpy as jnp
from jax import lax
from jax.experimental import pallas as pl
from jax.experimental.pallas import tpu as pltpu
from jax.sharding import PartitionSpec as P

D = 2560
HEAD_SIZE = 64
STATE = 128
KERNEL = 4
SPAN = 256
INNER = 5120


EPSILON = 1e-05
HIGH = lax.Precision.HIGHEST
HALF = lax.Precision.HIGH
LOW = -1e30
MESH = pl.DeviceIdType.MESH


def shifted(array, axis, by):
    length = lax.axis_size(axis)
    pairs = [(i, i + by) for i in range(length) if 0 <= i + by < length]
    return lax.ppermute(array, axis, pairs)


def rotated(array, axis, by):
    length = lax.axis_size(axis)
    return lax.ppermute(array, axis, [(i, (i + by) % length) for i in range(length)])


def sibling(array, axis):
    length = lax.axis_size(axis)
    return lax.ppermute(array, axis, [(i, i ^ 1) for i in range(length)])


def scattered_product(normed, weight, axis):
    length = lax.axis_size(axis)
    rank = lax.axis_index(axis)
    chips = length // 2
    share = weight.shape[1] // length

    def columns(core):
        return jnp.concatenate(
            [
                lax.dynamic_slice_in_dim(
                    weight, ((rank // 2 + by) % chips * 2 + core) * share, share, 1
                )
                for by in range(chips)
            ],
            axis=1,
        )

    theirs = columns(1 - rank % 2)
    ours = columns(rank % 2)
    other = jnp.dot(normed, theirs, preferred_element_type=jnp.float32)
    arrived = sibling(other, axis)
    pair = jnp.dot(normed, ours, preferred_element_type=jnp.float32) + arrived
    total = pair[:, :share]
    for by in range(1, chips):
        total = total + rotated(pair[:, by * share : (by + 1) * share], axis, 2 * by)
    return total


def gathered_features(part, axis):
    length = lax.axis_size(axis)
    rank = lax.axis_index(axis)
    chips = length // 2
    rows, share = part.shape
    column = [part] + [rotated(part, axis, 2 * by) for by in range(1, chips)]
    joined = jnp.concatenate(column, axis=1)
    twin = sibling(joined, axis)
    full = jnp.zeros((rows, share * length), part.dtype)
    for by in range(chips):
        source = (rank + 2 * (chips - by)) % length
        piece = slice(by * share, (by + 1) * share)
        full = lax.dynamic_update_slice_in_dim(full, joined[:, piece], source * share, 1)
        full = lax.dynamic_update_slice_in_dim(full, twin[:, piece], (source ^ 1) * share, 1)
    return full


def entering(through, state, axis):
    length = lax.axis_size(axis)
    tag = jnp.broadcast_to(through[:, None, None], (through.shape[0], 8, state.shape[2]))
    packed = shifted(jnp.concatenate([state, tag], axis=1), axis, 1)
    extent = state.shape[1]
    reach = 1
    while reach < length:
        earlier = shifted(packed, axis, reach)
        decay = packed[:, extent : extent + 1, :]
        packed = jnp.concatenate(
            [packed[:, :extent] + decay * earlier[:, :extent], decay * earlier[:, extent:]], axis=1
        )
        reach *= 2
    return packed[:, :extent]


def share_of(array):
    return array.shape[1] % TILE == 0


def document_of(positions, doc_lengths):
    starts = jnp.cumsum(doc_lengths) - doc_lengths
    return jnp.sum((positions[:, None] >= starts[None, :]).astype(jnp.int32), axis=1) - 1


def causal_conv(signal, rim_rows, weight, bias, positions, doc_ids, doc_lengths):
    length = signal.shape[0]
    taps = weight.shape[0]
    joined = jnp.concatenate([rim_rows, signal], axis=0).astype(jnp.float32)
    total = jnp.zeros(signal.shape, jnp.float32) + bias.astype(jnp.float32)[None, :]
    for offset in range(taps):
        lag = taps - 1 - offset
        source = document_of(positions - lag, doc_lengths)
        same = (source == doc_ids).astype(jnp.float32)
        total = (
            total
            + weight[offset].astype(jnp.float32)[None, :]
            * joined[offset : offset + length]
            * same[:, None]
        )
    return jax.nn.silu(total).astype(jnp.bfloat16)


def conv_state_kernel(x_ref, rim_ref, taps_ref, bias_ref, same_ref, cols_ref, bmat_ref, values_ref, state_ref, held):
    length, lanes = x_ref.shape
    taps = taps_ref.shape[0]
    held[0:8, :] = rim_ref[...].astype(jnp.float32)
    held[8:, :] = x_ref[...].astype(jnp.float32)
    total = jnp.zeros((length, lanes), jnp.float32) + bias_ref[...]
    for offset in range(taps):
        lag = taps - 1 - offset
        rows = held[8 - lag : 8 - lag + length, :]
        total = total + taps_ref[offset : offset + 1, :] * rows * same_ref[:, lag : lag + 1]
    values = jax.nn.silu(total).astype(jnp.bfloat16)
    values_ref[...] = values
    first = lax.broadcasted_iota(jnp.int32, (length, lanes), 1) < HEAD_SIZE
    tail = jnp.where(first, cols_ref[0, :, 2:3], cols_ref[0, :, 3:4])
    scaled = values.astype(jnp.float32) * tail
    high = scaled.astype(jnp.bfloat16)
    low = (scaled - high.astype(jnp.float32)).astype(jnp.bfloat16)
    bmat = bmat_ref[...]
    dims = (((0,), (0,)), ((), ()))
    state_ref[...] = lax.dot_general(
        high, bmat, dims, preferred_element_type=jnp.float32
    ) + lax.dot_general(low, bmat, dims, preferred_element_type=jnp.float32)


def within_kernel(values_ref, scores_ref, cols_ref, rows_ref, skip_ref, out_ref):
    length, lanes = values_ref.shape
    for cut in range(0, length, SPAN):
        upto = cut + SPAN
        values = values_ref[0:upto, :]
        scores = scores_ref[cut:upto, 0:upto]
        parts = []
        for which in range(2):
            gap = rows_ref[0, which : which + 1, 0:upto] - cols_ref[0, cut:upto, which : which + 1]
            weights = (
                jnp.exp(jnp.minimum(gap, 0.0)) * scores * rows_ref[0, 2 + which : 3 + which, 0:upto]
            )
            high = weights.astype(jnp.bfloat16)
            low = (weights - high.astype(jnp.float32)).astype(jnp.bfloat16)
            parts.append(
                jnp.dot(high, values, preferred_element_type=jnp.float32)
                + jnp.dot(low, values, preferred_element_type=jnp.float32)
            )
        first = lax.broadcasted_iota(jnp.int32, (SPAN, lanes), 1) < HEAD_SIZE
        own = values_ref[cut:upto, :].astype(jnp.float32)
        out_ref[cut:upto, :] = jnp.where(first, parts[0], parts[1]) + skip_ref[...] * own


def conv_state(x_in, rim, taps, bias, same, cols, bmat):
    length, inner_here = x_in.shape
    lanes = 2 * HEAD_SIZE
    return pl.pallas_call(
        conv_state_kernel,
        grid=(inner_here // lanes,),
        in_specs=[
            pl.BlockSpec((length, lanes), lambda i: (0, i)),
            pl.BlockSpec((8, lanes), lambda i: (0, i)),
            pl.BlockSpec((taps.shape[0], lanes), lambda i: (0, i)),
            pl.BlockSpec((1, lanes), lambda i: (0, i)),
            pl.BlockSpec(same.shape, lambda i: (0, 0)),
            pl.BlockSpec((1, length, 4), lambda i: (i, 0, 0)),
            pl.BlockSpec(bmat.shape, lambda i: (0, 0)),
        ],
        out_specs=[
            pl.BlockSpec((length, lanes), lambda i: (0, i)),
            pl.BlockSpec((lanes, STATE), lambda i: (i, 0)),
        ],
        out_shape=[
            jax.ShapeDtypeStruct((length, inner_here), jnp.bfloat16),
            jax.ShapeDtypeStruct((inner_here, STATE), jnp.float32),
        ],
        scratch_shapes=[pltpu.VMEM((length + 8, lanes), jnp.float32)],
        cost_estimate=pl.CostEstimate(flops=10**9, bytes_accessed=6 * 10**6, transcendentals=10**6),
    )(x_in, rim, taps, bias, same, cols, bmat)


def within(values, scores, cols, rows, skip):
    length, inner_here = values.shape
    lanes = 2 * HEAD_SIZE
    return pl.pallas_call(
        within_kernel,
        grid=(inner_here // lanes,),
        in_specs=[
            pl.BlockSpec((length, lanes), lambda i: (0, i)),
            pl.BlockSpec(scores.shape, lambda i: (0, 0)),
            pl.BlockSpec((1, length, 4), lambda i: (i, 0, 0)),
            pl.BlockSpec((1, 4, length), lambda i: (i, 0, 0)),
            pl.BlockSpec((1, lanes), lambda i: (0, i)),
        ],
        out_specs=pl.BlockSpec((length, lanes), lambda i: (0, i)),
        out_shape=jax.ShapeDtypeStruct((length, inner_here), jnp.float32),
        cost_estimate=pl.CostEstimate(flops=8 * 10**9, bytes_accessed=20 * 10**6, transcendentals=10**7),
    )(values, scores, cols, rows, skip)


TAIL_ROWS = 256
TILE = 128


def tail_kernel(
    n, heads, first_of, hid_ref, tgt_ref, member_ref, w_ref, out_ref,
    full, w_buf, tgts, marks, parts, sums,
    w_sem, along_send, side_send, arrive, tgt_send, tgt_recv, mark_send, mark_recv, sum_send, sum_recv,
):
    z = lax.axis_index("seq")
    h = lax.axis_index("head")
    rows, share = hid_ref.shape
    width = w_ref.shape[1]
    total_peers = n * heads
    me = z * heads + h
    twin = h + 1 - 2 * lax.rem(h, 2)
    side = lax.rem(h + 2, heads)

    load = pltpu.make_async_copy(w_ref, w_buf, w_sem)
    load.start()
    barrier = pltpu.get_barrier_semaphore()

    def peer(k):
        flat = lax.rem(me + k, total_peers)
        return flat // heads, lax.rem(flat, heads)

    @pl.loop(1, total_peers)
    def _(k):
        there, where_head = peer(k)
        pl.semaphore_signal(
            barrier, inc=1, device_id={"seq": there, "head": where_head}, device_id_type=MESH
        )

    pl.semaphore_wait(barrier, total_peers - 1)

    def slot(block, head):
        return full.at[block, :, pl.ds(pl.multiple_of(head * share, TILE), share)]

    def ship(kind, block, head, target, source=None):
        sem = along_send if kind < 2 else side_send
        return pltpu.make_async_remote_copy(
            src_ref=slot(block, head) if source is None else source,
            dst_ref=slot(block, head),
            send_sem=sem.at[kind % 2, block, head] if kind < 2 else sem.at[kind - 2, block, head],
            recv_sem=arrive.at[block, head],
            device_id=target,
            device_id_type=MESH,
        )

    def right(block, source=None):
        return ship(0, block, h, {"seq": z + 1}, source)

    def left(block, source=None):
        return ship(1, block, h, {"seq": z - 1}, source)

    def across(block, source=None):
        return ship(2, block, h, {"head": side}, source)

    def twinned(block, head, source=None):
        return ship(3, block, head, {"head": twin}, source)

    def arrived(block, head):
        ship(0, block, head, {"head": twin}).wait_recv()

    def tell(k):
        return pltpu.make_async_remote_copy(
            src_ref=tgt_ref,
            dst_ref=tgts.at[z],
            send_sem=tgt_send.at[k],
            recv_sem=tgt_recv.at[z],
            device_id={"seq": lax.rem(z + k, n)},
            device_id_type=MESH,
        )

    across(z, hid_ref).start()

    @pl.when(z < n - 1)
    def _():
        right(z, hid_ref).start()

    @pl.when(z > 0)
    def _():
        left(z, hid_ref).start()

    twinned(z, h, hid_ref).start()
    for k in range(1, n):
        tell(k).start()
    tgts[z] = tgt_ref[...]
    full[z, :, pl.ds(pl.multiple_of(h * share, TILE), share)] = hid_ref[...]
    load.wait()

    def mark_copy(block, head):
        return pltpu.make_async_remote_copy(
            src_ref=marks.at[block, :, pl.ds(pl.multiple_of(head * TILE, TILE), TILE)],
            dst_ref=parts.at[me],
            send_sem=mark_send.at[block, head],
            recv_sem=mark_recv.at[me],
            device_id={"seq": block, "head": head},
            device_id_type=MESH,
        )

    def compute(block):
        dead, first = first_of(z, h, width)

        @pl.loop(0, rows // TAIL_ROWS)
        def _(step):
            at = pl.multiple_of(step * TAIL_ROWS, TAIL_ROWS)
            logits = jnp.dot(
                full[block, pl.ds(at, TAIL_ROWS), :], w_buf[...], preferred_element_type=jnp.float32
            )
            wanted = tgts[block, 0:1, pl.ds(at, TAIL_ROWS)]
            wanted = jnp.transpose(jnp.broadcast_to(wanted, (TILE, TAIL_ROWS))) - first
            lane = lax.broadcasted_iota(jnp.int32, (TAIL_ROWS, TILE), 1)
            pieces = []
            for cut in range(0, width, TILE):
                piece = logits[:, cut : cut + TILE]
                pieces.append(jnp.where(lane + cut >= dead, piece, LOW))
            peak = pieces[0]
            for piece in pieces[1:]:
                peak = jnp.maximum(peak, piece)
            peak = jnp.max(peak, axis=1, keepdims=True)
            total = jnp.zeros((TAIL_ROWS, TILE), jnp.float32)
            picked = jnp.zeros((TAIL_ROWS, TILE), jnp.float32)
            for index, piece in enumerate(pieces):
                total = total + jnp.exp(piece - peak)
                here = (lane + index * TILE == wanted) & (lane + index * TILE >= dead)
                picked = picked + jnp.where(here, piece, 0.0)
            total = jnp.sum(total, axis=1, keepdims=True)
            picked = jnp.sum(picked, axis=1, keepdims=True)
            tile = jnp.where(lane == 0, peak, jnp.where(lane == 1, total, picked))
            marks[block, :, pl.ds(at, TAIL_ROWS)] = jnp.transpose(tile)[0:8, :]

        @pl.loop(0, heads)
        def _(head):
            @pl.when((block != z) | (head != h))
            def _():
                mark_copy(block, head).start()

    def finish(block):
        arrived(block, side)
        twinned(block, side).start()
        arrived(block, twin)
        arrived(block, lax.rem(twin + 2, heads))
        compute(block)

    for step in range(1, n):
        @pl.when(z >= step)
        def _():
            block = z - step
            arrived(block, h)

            @pl.when(z < n - 1)
            def _():
                right(block).start()

            across(block).start()
            twinned(block, h).start()

        @pl.when(z + step < n)
        def _():
            block = z + step
            arrived(block, h)

            @pl.when(z > 0)
            def _():
                left(block).start()

            across(block).start()
            twinned(block, h).start()

        if step == 1:
            for k in range(1, n):
                source = lax.rem(z + n - k, n)
                pltpu.make_async_remote_copy(
                    src_ref=tgt_ref,
                    dst_ref=tgts.at[source],
                    send_sem=tgt_send.at[k],
                    recv_sem=tgt_recv.at[source],
                    device_id={"seq": lax.rem(z + k, n)},
                    device_id_type=MESH,
                ).wait()
            finish(z)
        else:
            @pl.when(z >= step - 1)
            def _():
                finish(z - step + 1)

            @pl.when(z + step - 1 < n)
            def _():
                finish(z + step - 1)

    if n > 1:
        @pl.when(z >= n - 1)
        def _():
            finish(z - n + 1)

        @pl.when(z + n - 1 < n)
        def _():
            finish(z + n - 1)

    parts[me] = marks[z, :, pl.ds(pl.multiple_of(h * TILE, TILE), TILE)]

    def mark_arrival(k):
        there, where_head = peer(k)
        flat = there * heads + where_head
        pltpu.make_async_remote_copy(
            src_ref=parts.at[flat],
            dst_ref=parts.at[flat],
            send_sem=mark_send.at[there, where_head],
            recv_sem=mark_recv.at[flat],
            device_id={"seq": there, "head": where_head},
            device_id_type=MESH,
        ).wait()

    @pl.loop(1, total_peers)
    def _(k):
        mark_arrival(k)

    peak = parts[0, 0:1, :]
    for flat in range(1, total_peers):
        peak = jnp.maximum(peak, parts[flat, 0:1, :])
    total = jnp.zeros((1, TILE), jnp.float32)
    picked = jnp.zeros((1, TILE), jnp.float32)
    for flat in range(total_peers):
        total = total + parts[flat, 1:2, :] * jnp.exp(parts[flat, 0:1, :] - peak)
        picked = picked + parts[flat, 2:3, :]
    losses = peak + jnp.log(total) - picked
    mine = jnp.sum(member_ref[...] * losses, axis=1, keepdims=True)
    sums[me] = jnp.broadcast_to(mine, sums.shape[1:])

    def sum_copy(k, slot_of):
        there, where_head = peer(k)
        return pltpu.make_async_remote_copy(
            src_ref=sums.at[slot_of],
            dst_ref=sums.at[slot_of],
            send_sem=sum_send.at[k],
            recv_sem=sum_recv.at[slot_of],
            device_id={"seq": there, "head": where_head},
            device_id_type=MESH,
        )

    @pl.loop(1, total_peers)
    def _(k):
        sum_copy(k, me).start()

    for block in range(n):
        @pl.when((z < n - 1) & (z >= block))
        def _():
            right(block).wait_send()

        @pl.when((z > 0) & (z <= block))
        def _():
            left(block).wait_send()

        across(block).wait_send()
        twinned(block, h).wait_send()
        twinned(block, side).wait_send()

    @pl.loop(1, total_peers)
    def _(k):
        sum_copy(k, lax.rem(me + k, total_peers)).wait()

    grand = sums[0]
    for flat in range(1, total_peers):
        grand = grand + sums[flat]
    out_ref[...] = grand


def loss_stage(hidden_part, targets_row, member, weight, n, heads, first_of):
    rows, _ = hidden_part.shape
    deep, width = weight.shape
    peers = n * heads
    dma = pltpu.SemaphoreType.DMA
    flops = 2 * n * rows * deep * width
    return pl.pallas_call(
        functools.partial(tail_kernel, n, heads, first_of),
        out_shape=jax.ShapeDtypeStruct(member.shape, jnp.float32),
        in_specs=[pl.BlockSpec(memory_space=pltpu.VMEM)] * 3 + [pl.BlockSpec(memory_space=pl.ANY)],
        out_specs=pl.BlockSpec(memory_space=pltpu.VMEM),
        scratch_shapes=[
            pltpu.VMEM((n, rows, deep), jnp.bfloat16),
            pltpu.VMEM((deep, width), jnp.bfloat16),
            pltpu.VMEM((n, 8, rows), jnp.int32),
            pltpu.VMEM((n, 8, rows), jnp.float32),
            pltpu.VMEM((peers, 8, TILE), jnp.float32),
            pltpu.VMEM((peers,) + member.shape, jnp.float32),
            dma,
            dma((2, n, heads)),
            dma((2, n, heads)),
            dma((n, heads)),
            dma((n,)),
            dma((n,)),
            dma((n, heads)),
            dma((peers,)),
            dma((peers,)),
            dma((peers,)),
        ],
        compiler_params=pltpu.CompilerParams(
            collective_id=0, has_side_effects=True, vmem_limit_bytes=60 * 2**20
        ),
        cost_estimate=pl.CostEstimate(
            flops=flops, bytes_accessed=deep * width * 2, transcendentals=n * rows * width
        ),
    )(hidden_part, targets_row, member, weight)


def local(
    residual,
    x_in,
    bc_in,
    z_in,
    dt_raw,
    dt_bias,
    decay_rate,
    d_skip,
    conv_x_weight,
    conv_x_bias,
    conv_bc_weight,
    conv_bc_bias,
    norm_gain,
    out_weight,
    final_gain,
    lm_weight,
    targets,
    doc_lengths,
):
    length = x_in.shape[0]
    inner_here = x_in.shape[1]
    heads_here = dt_raw.shape[0]
    seq_rank = lax.axis_index("seq")
    head_rank = lax.axis_index("head")
    offset_here = seq_rank * length
    positions = offset_here + jnp.arange(length, dtype=jnp.int32)
    doc_ids = document_of(positions, doc_lengths)
    columns_here = lm_weight.shape[1]
    devices = lax.axis_size("seq")
    width = -(-columns_here // (devices * 128)) * 128

    def window(rank):
        return jnp.minimum(rank * width, columns_here - width)

    depth = lm_weight.shape[0]
    vocab_weight = jnp.zeros((depth * devices, width), lm_weight.dtype)
    group = lax.axis_index("groups")
    groups = lax.axis_size("groups")
    band = depth // groups
    pieces = [
        lax.dynamic_slice(
            lm_weight, (group * band, window((seq_rank + by) % devices)), (band, width)
        )
        for by in range(1, devices)
    ]
    heads = lax.axis_size("head")
    room = 2 * (devices * length * D + D * width) < 40 * 2**20
    fused = room and heads == 4 and length == heads * TILE and share_of(residual) and devices > 1
    aims = [targets]
    for by in range(1, 1 if fused else devices):
        aims.append(rotated(targets, "seq", by))
    margin = KERNEL - 1
    rims = shifted(
        jnp.concatenate([x_in[length - margin :], bc_in[length - margin :]], axis=1), "seq", 1
    )
    x_rim, bc_rim = rims[:, :inner_here], rims[:, inner_here:]
    keys_queries = causal_conv(
        bc_in, bc_rim, conv_bc_weight, conv_bc_bias, positions, doc_ids, doc_lengths
    )
    bmat, cmat = keys_queries[:, :STATE], keys_queries[:, STATE:]
    steps = jax.nn.softplus(dt_raw + dt_bias[:, None])
    climb = jnp.cumsum(steps * decay_rate[:, None], axis=1)
    before = document_of(jnp.reshape(offset_here - 1, (1,)), doc_lengths)[0]
    carried = (doc_ids == before).astype(jnp.float32)
    through = jnp.exp(-climb[:, length - 1]) * carried[length - 1]
    same = jnp.stack(
        [
            (document_of(positions - lag, doc_lengths) == doc_ids).astype(jnp.float32)
            for lag in range(KERNEL)
        ],
        axis=1,
    )
    last = (doc_ids == doc_ids[length - 1]).astype(jnp.float32)
    tail = jnp.exp(climb - climb[:, length - 1 :]) * last[None, :] * steps
    couples = heads_here // 2
    rows = jnp.concatenate(
        [climb.reshape(couples, 2, length), steps.reshape(couples, 2, length)], axis=1
    )
    cols = jnp.concatenate(
        [climb.reshape(couples, 2, length), tail.reshape(couples, 2, length)], axis=1
    ).transpose(0, 2, 1)
    rim = jnp.concatenate([jnp.zeros((8 - margin, inner_here), x_rim.dtype), x_rim], axis=0)
    values, own_end = conv_state(
        x_in,
        rim,
        conv_x_weight.astype(jnp.float32),
        conv_x_bias.astype(jnp.float32)[None, :],
        same,
        cols,
        bmat,
    )
    of_head = jnp.arange(inner_here, dtype=jnp.int32)[None, :] // HEAD_SIZE
    spread = (of_head == jnp.arange(heads_here, dtype=jnp.int32)[:, None]).astype(jnp.float32)
    incoming = entering(
        through, own_end.reshape(heads_here, HEAD_SIZE, STATE), "seq"
    ).reshape(inner_here, STATE)
    held_back = lax.optimization_barrier(tuple(pieces[1:]) + (incoming,))
    pieces, incoming = pieces[:1] + list(held_back[:-1]), held_back[-1]
    arrivals = []
    for by in range(1, devices):
        arrivals.append(rotated(pieces[by - 1], "seq", by))
    bands = []
    for by in range(1, devices):
        bands.append(
            [arrivals[by - 1]]
            + [rotated(arrivals[by - 1], "groups", hop) for hop in range(1, groups)]
        )
    order = jnp.arange(length, dtype=jnp.int32)
    inside = (doc_ids[:, None] == doc_ids[None, :]) & (order[:, None] >= order[None, :])
    scores = jnp.where(
        inside,
        lax.dot_general(
            cmat, bmat, (((1,), (1,)), ((), ())), preferred_element_type=jnp.float32
        ),
        0.0,
    )
    skip = jnp.dot(d_skip[None, :], spread, precision=HIGH)
    output = within(values, scores, cols, rows, skip)
    entry = jnp.dot((jnp.exp(-climb) * carried[None, :]).T, spread, precision=HIGH)
    arriving = lax.dot_general(
        cmat.astype(jnp.float32), incoming, (((1,), (1,)), ((), ())), precision=HALF
    )
    gated = (output + arriving * entry) * jax.nn.silu(z_in.astype(jnp.float32))
    square_sum = lax.psum(jnp.sum(gated * gated, axis=1), "head")
    scale = lax.rsqrt(square_sum / INNER + EPSILON)
    normed = (gated * scale[:, None] * norm_gain.astype(jnp.float32)[None, :]).astype(jnp.bfloat16)
    share = residual.shape[1]
    projected = scattered_product(normed, out_weight, "head")
    block_out = (residual.astype(jnp.float32) + projected).astype(jnp.bfloat16)
    widened = block_out.astype(jnp.float32)
    square_total = lax.psum(jnp.sum(widened * widened, axis=1), "head")
    gain_part = lax.dynamic_slice_in_dim(final_gain, head_rank * share, share, 0)
    final_scale = lax.rsqrt(square_total / D + EPSILON)
    hidden_part = (widened * final_scale[:, None] * gain_part.astype(jnp.float32)[None, :]).astype(
        jnp.bfloat16
    )
    own = lax.dynamic_slice_in_dim(lm_weight, window(seq_rank), width, 1)
    vocab_weight = lax.dynamic_update_slice_in_dim(vocab_weight, own, seq_rank * depth, 0)
    for by in range(1, devices):
        source = (seq_rank + devices - by) % devices
        for hop in range(groups):
            start = source * depth + (group + groups - hop) % groups * band
            vocab_weight = lax.dynamic_update_slice_in_dim(
                vocab_weight, bands[by - 1][hop], start, 0
            )
    if fused:
        documents = -(-doc_lengths.shape[0] // 8) * 8
        own_ids = lax.dynamic_slice_in_dim(doc_ids, head_rank * TILE, TILE, 0)
        member = (own_ids[None, :] == jnp.arange(documents, dtype=jnp.int32)[:, None]).astype(
            jnp.float32
        )

        def first_of(z, h, wide):
            start = jnp.minimum(z * wide, columns_here - wide)
            return z * wide - start, h * columns_here + start

        row = jnp.broadcast_to(targets[None, :], (8, length))
        sums = loss_stage(hidden_part, row, member, vocab_weight, devices, heads, first_of)
        sums = sums[: doc_lengths.shape[0], 0]
        return (block_out, sums / doc_lengths.astype(jnp.float32))
    column = jnp.arange(width, dtype=jnp.int32)
    first = head_rank * columns_here + window(seq_rank)
    live = column + window(seq_rank) >= seq_rank * width
    marks = jnp.zeros((3, length * devices), jnp.float32)
    for by in range(devices):
        source = (seq_rank + devices - by) % devices
        if by and by % 4 == 0:
            hidden_part, marks = lax.optimization_barrier((hidden_part, marks))
        rows = rotated(hidden_part, "seq", by) if by else hidden_part
        hidden = gathered_features(rows, "head")
        logits = jnp.dot(hidden, vocab_weight, preferred_element_type=jnp.float32)
        logits = jnp.where(live[None, :], logits, LOW)
        peak = jnp.max(logits, axis=1)
        wanted = aims[by] - first
        total = jnp.sum(jnp.exp(logits - peak[:, None]), axis=1)
        picked = jnp.sum(
            jnp.where((column[None, :] == wanted[:, None]) & live[None, :], logits, 0.0), axis=1
        )
        marks = lax.dynamic_update_slice_in_dim(
            marks, jnp.stack([peak, total, picked]), source * length, 1
        )
    for axis in ("head", "seq"):
        every_mark = lax.all_gather(marks, axis)
        peak = jnp.max(every_mark[:, 0], axis=0)
        total = jnp.sum(every_mark[:, 1] * jnp.exp(every_mark[:, 0] - peak[None]), axis=0)
        marks = jnp.stack([peak, total, jnp.sum(every_mark[:, 2], axis=0)])
    losses = marks[0] + jnp.log(marks[1]) - marks[2]
    every = document_of(jnp.arange(length * devices, dtype=jnp.int32), doc_lengths)
    documents = jnp.arange(doc_lengths.shape[0], dtype=jnp.int32)
    member = every[None, :] == documents[:, None]
    sums = jnp.sum(jnp.where(member, losses[None, :], 0.0), axis=1)
    return (block_out, sums / doc_lengths.astype(jnp.float32))


def solution(mesh):
    in_specs = (
        P(("groups", "seq"), "head"),
        P(("groups", "seq"), "head"),
        P(("groups", "seq"), None),
        P(("groups", "seq"), "head"),
        P("head", ("groups", "seq")),
        P("head"),
        P("head"),
        P("head"),
        P(None, "head"),
        P("head"),
        P(),
        P(),
        P("head"),
        P("head", None),
        P(),
        P("seq", "head"),
        P(("groups", "seq")),
        P("groups"),
    )
    out_specs = (P(("groups", "seq"), "head"), P("groups"))


    return jax.shard_map(local, mesh=mesh, in_specs=in_specs, out_specs=out_specs, check_vma=False)
```

profile of v0, /device:TPU:0, one launch (start us, length us, event | category | flops | bytes accessed | tf_op | source)
XLA Modules:
  0.0 360.1 jit_solution(7702701666362973751)
XLA Ops:
  2.2 5.0 %collective-permute-start = (bf16[3,1536]{1,0:T(4,128)(2,1)S(1)}, bf16[3,1536]{1,0:T(4,128)(2,1)S(1)}, u32[]{:S(2)}, u32[]{:S(2)}) collective-permute-start(bf16[3,1536]{1,0:T(4,128)(2,1)S(1)} %pad_maximum_fusion.4), channel_id=1, source_target_pairs={{0,4},{4,8},{8,12},{1,5},{5,9},{9,13},{2,6},{6,10},{10,14},{3,7},{... | collective-permute-start | bytes 27656 | tf_op jit(solution)/shard_map/ppermute | solution.py:28
  20.4 2.3 copy.42.cols_ref
  24.5 11.0 %shard_map.185 = (bf16[512,1280]{1,0:T(8,128)(2,1)}, f32[1280,128]{1,0:T(8,128)}) custom-call(bf16[512,1280]{1,0:T(8,128)(2,1)} %x_ref.1, bf16[8,1280]{1,0:T(8,128)(2,1)} %concatenate.28.rim_ref, f32[4,1280]{1,0:T(4,128)} %convert_element_type.144.taps_ref, f32[1,1280]{1,0:T(1,128)} %reshape.229.bias_ref, f32[512,4]{1,0:T(8,128)} %copy.41.same_ref, ...), custom_call_target="tpu_custom_call" | custom-call | flops 1000000000 | bytes 6000000 | tf_op jit(solution)/shard_map/pallas_call | solution.py:179
  36.7 3.5 collective-permute-start.1
  41.2 5.6 %fusion.54 = (bf16[320,1664]{1,0:T(8,128)(2,1)}, bf16[320,1664]{1,0:T(8,128)(2,1)}, bf16[320,1664]{1,0:T(8,128)(2,1)}) fusion(bf16[640,6400]{1,0:T(8,128)(2,1)} %param.33, s32[]{:T(128)S(6)} %select_n.141, s32[]{:T(128)S(6)} %select_n.159, s32[]{:T(128)S(6)} %select_n.145, s32[]{:T(128)S(6)} %select_n.143), kind=kLoop, calls=%fused_computation.126 | loop fusion | bytes 6389776 | tf_op jit(solution)/shard_map/dynamic_slice | solution.py:570
  46.8 8.9 %collective-permute-done.1 = f32[20,72,128]{2,1,0:T(8,128)S(1)} collective-permute-done((f32[20,72,128]{2,1,0:T(8,128)S(1)}, f32[20,72,128]{2,1,0:T(8,128)S(1)}, u32[]{:S(2)}, u32[]{:S(2)}) %collective-permute-start.1) | collective-permute-done | bytes 737312 | tf_op jit(solution)/shard_map/ppermute | solution.py:28
  55.7 4.4 %collective-permute-start.2 = (f32[20,72,128]{2,1,0:T(8,128)S(1)}, f32[20,72,128]{2,1,0:T(8,128)S(1)}, u32[]{:S(2)}, u32[]{:S(2)}) collective-permute-start(f32[20,72,128]{2,1,0:T(8,128)S(1)} %collective-permute-done.1), channel_id=1, source_target_pairs={{0,4},{4,8},{8,12},{1,5},{5,9},{9,13},{2,6},{6,10},{10,14},{3,7},{... | collective-permute-start | bytes 2211848 | tf_op jit(solution)/shard_map/ppermute | solution.py:28
  60.1 5.8 %constant_dynamic-slice_fusion.3 = (bf16[1280,640]{1,0:T(8,128)(2,1)}, bf16[1280,640]{1,0:T(8,128)(2,1)}, bf16[1280,640]{1,0:T(8,128)(2,1)}, bf16[1280,640]{1,0:T(8,128)(2,1)}) fusion(bf16[1280,2560]{1,0:T(8,128)(2,1)} %param.31, s32[]{:T(128)S(6)} %select_n.149, s32[]{:T(128)S(6)} %select_n.151, s32[]{:T(128)S(6)} %select_n.153, s32[]{:T(128)S(6)} %select_n.152), kind=kLoop, calls=%fused_computation.95 | loop fusion | bytes 13107216 | tf_op jit(solution)/shard_map/dynamic_slice | solution.py:50
  67.2 7.4 %collective-permute-done.2 = f32[20,72,128]{2,1,0:T(8,128)S(1)} collective-permute-done((f32[20,72,128]{2,1,0:T(8,128)S(1)}, f32[20,72,128]{2,1,0:T(8,128)S(1)}, u32[]{:S(2)}, u32[]{:S(2)}) %collective-permute-start.2) | collective-permute-done | bytes 737312 | tf_op jit(solution)/shard_map/ppermute | solution.py:28
  74.8 5.4 %collective-permute-start.3 = (f32[20,72,128]{2,1,0:T(8,128)S(1)}, f32[20,72,128]{2,1,0:T(8,128)S(1)}, u32[]{:S(2)}, u32[]{:S(2)}) collective-permute-start(f32[20,72,128]{2,1,0:T(8,128)S(1)} %pad_maximum_fusion.1), channel_id=1, source_target_pairs={{0,8},{4,12},{1,9},{5,13},{2,10},{6,14},{3,11},{7,15},{16,24},{20,... | collective-permute-start | bytes 2211848 | tf_op jit(solution)/shard_map/ppermute | solution.py:28
  80.3 12.0 %shard_map.186 = f32[512,1280]{1,0:T(8,128)} custom-call(bf16[512,1280]{1,0:T(8,128)(2,1)} %get-tuple-element.7.values_ref, f32[512,512]{1,0:T(8,128)} %convolution_select_fusion.scores_ref, f32[10,512,4]{2,1,0:T(8,128)} %copy.42.cols_ref, f32[10,4,512]{2,1,0:T(4,128)} %get-tuple-element.31.rows_ref, f32[1,1280]{1,0:T(1,128)} %fusion.26.skip_ref), custom_call_target="tpu_custom_call" | custom-call | flops 8000000000 | bytes 20000000 | tf_op jit(solution)/shard_map/pallas_call | solution.py:207
  92.3 1.7 collective-permute-done.3
  98.3 5.8 %psum.14 = f32[512]{0:T(512)S(1)} all-reduce(f32[512]{0:T(512)S(1)} %get-tuple-element.18), channel_id=1, replica_groups=mesh['groups'=2,'seq'=4,'head'=4] {'head'}, use_global_device_ids=true, to_apply=%region_9.10 | all-reduce | flops 512 | bytes 4096 | tf_op jit(solution)/shard_map/psum | solution.py:653
  104.2 5.5 %fusion.3 = f32[512,1280]{1,0:T(8,128)} fusion(bf16[1280,640]{1,0:T(8,128)(2,1)} %get-tuple-element.29, bf16[1280,640]{1,0:T(8,128)(2,1)} %get-tuple-element.30, f32[512,1280]{1,0:T(8,128)S(1)} %get-tuple-element.19, f32[1280]{0:T(1024)S(1)} %convert_element_type.165, f32[512]{0:T(512)S(1)} %add_rsqrt_fusion.1), kind=kOutput, calls=%fused_computation.5 | convolution fusion | flops 1686241280 | bytes 8526848 | tf_op jit(solution)/shard_map/dot_general | solution.py:60
  109.6 17.1 %collective-permute-start.6 = (bf16[320,1664]{1,0:T(8,128)(2,1)}, bf16[320,1664]{1,0:T(8,128)(2,1)}, u32[]{:S(2)}, u32[]{:S(2)}) collective-permute-start(bf16[320,1664]{1,0:T(8,128)(2,1)} %get-tuple-element.24), channel_id=1, source_target_pairs={{0,4},{4,8},{8,12},{12,0},{1,5},{5,9},{9,13},{13,1},{2,6},{6,10},{... | collective-permute-start | bytes 3194888 | tf_op jit(solution)/shard_map/ppermute | solution.py:33
  126.7 3.4 collective-permute-start.8
  130.1 3.9 %broadcast_in_dim.18 = bf16[2560,1664]{1,0:T(8,128)(2,1)} broadcast(bf16[]{:T(256)} %constant.170.clone.1), dimensions={} | broadcast | bytes 8519682 | tf_op jit(solution)/shard_map/broadcast_in_dim | solution.py:565
  134.0 3.9 %dynamic-slice_dynamic-update-slice_fusion = bf16[2560,1664]{1,0:T(8,128)(2,1)} fusion(bf16[2560,1664]{1,0:T(8,128)(2,1)} %broadcast_in_dim.18, s32[]{:T(128)S(6)} %select_n.157, bf16[640,6400]{1,0:T(8,128)(2,1)} %param.33, s32[]{:T(128)S(6)} %select_n.156), kind=kLoop, calls=%fused_computation.17 | loop fusion | bytes 4259848 | tf_op jit(solution)/shard_map/dynamic_update_slice | solution.py:667
  137.9 16.5 %collective-permute-done.6 = bf16[320,1664]{1,0:T(8,128)(2,1)} collective-permute-done((bf16[320,1664]{1,0:T(8,128)(2,1)}, bf16[320,1664]{1,0:T(8,128)(2,1)}, u32[]{:S(2)}, u32[]{:S(2)}) %collective-permute-start.6) | collective-permute-done | bytes 1064992 | tf_op jit(solution)/shard_map/ppermute | solution.py:33
  154.3 1.5 collective-permute-start.7
  157.3 42.4 %collective-permute-done.8 = bf16[320,1664]{1,0:T(8,128)(2,1)} collective-permute-done((bf16[320,1664]{1,0:T(8,128)(2,1)}, bf16[320,1664]{1,0:T(8,128)(2,1)}, u32[]{:S(2)}, u32[]{:S(2)}) %collective-permute-start.8) | collective-permute-done | bytes 1064992 | tf_op jit(solution)/shard_map/ppermute | solution.py:33
  199.7 1.5 collective-permute-start.9
  201.8 4.7 %convolution_add_fusion = f32[512,1280]{1,0:T(8,128)S(1)} fusion(f32[512,1280]{1,0:T(8,128)} %collective-permute-done.4, bf16[1280,640]{1,0:T(8,128)(2,1)} %get-tuple-element.28, bf16[1280,640]{1,0:T(8,128)(2,1)} %get-tuple-element.27, f32[512,1280]{1,0:T(8,128)S(1)} %get-tuple-element.19, f32[1280]{0:T(1024)S(1)} %convert_element_type.165, ...), kind=kOutput, calls=%fused_computation.1 | convolution fusion | flops 1686896640 | bytes 11148288 | tf_op jit(solution)/shard_map/dot_general | solution.py:62
  206.6 1.3 collective-permute-start.5
  207.9 2.3 constant_dynamic-update-slice_fusion.4
  210.2 2.3 constant_dynamic-update-slice_fusion.3
  212.5 2.3 constant_dynamic-update-slice_fusion.2
  214.8 11.5 %collective-permute-done.9 = bf16[320,1664]{1,0:T(8,128)(2,1)S(1)} collective-permute-done((bf16[320,1664]{1,0:T(8,128)(2,1)}, bf16[320,1664]{1,0:T(8,128)(2,1)S(1)}, u32[]{:S(2)}, u32[]{:S(2)}) %collective-permute-start.9) | collective-permute-done | bytes 1064992 | tf_op jit(solution)/shard_map/ppermute | solution.py:33
  227.4 2.4 constant_dynamic-update-slice_fusion
  229.8 18.4 %collective-permute-done.11 = bf16[320,1664]{1,0:T(8,128)(2,1)S(1)} collective-permute-done((bf16[320,1664]{1,0:T(8,128)(2,1)}, bf16[320,1664]{1,0:T(8,128)(2,1)S(1)}, u32[]{:S(2)}, u32[]{:S(2)}) %collective-permute-start.11) | collective-permute-done | bytes 1064992 | tf_op jit(solution)/shard_map/ppermute | solution.py:33
  249.7 5.7 %psum.15 = f32[512]{0:T(512)S(1)} all-reduce(f32[512]{0:T(512)S(1)} %get-tuple-element.16), channel_id=1, replica_groups=mesh['groups'=2,'seq'=4,'head'=4] {'head'}, use_global_device_ids=true, to_apply=%region_11.12 | all-reduce | flops 512 | bytes 4096 | tf_op jit(solution)/shard_map/psum | solution.py:660
  257.1 101.7 %shard_map.187 = f32[8,128]{1,0:T(8,128)} custom-call(bf16[512,640]{1,0:T(8,128)(2,1)} %fusion.13.hid_ref, s32[8,512]{1,0:T(8,128)} %broadcast_in_dim.17.tgt_ref, f32[8,128]{1,0:T(8,128)} %fusion.40.member_ref, bf16[2560,1664]{1,0:T(8,128)(2,1)} %constant_dynamic-update-slice_fusion.5.w_ref), custom_call_target="tpu_custom_call" | custom-call | flops 17448304640 | bytes 8519680 | tf_op jit(solution)/shard_map/pallas_call | solution.py:497
  (103 shorter events, 31.1 us)
Async XLA Ops:
  0.6 39.8 %copy-start = (f32[20]{0:T(128)S(1)}, f32[20]{0:T(128)}, u32[]{:S(2)}) copy-start(f32[20]{0:T(128)} %param.25) | copy-start | bytes 244
  0.6 22.1 %copy-start.6 = (bf16[512,256]{1,0:T(8,128)(2,1)S(1)}, bf16[512,256]{1,0:T(8,128)(2,1)}, u32[]{:S(2)}) copy-start(bf16[512,256]{1,0:T(8,128)(2,1)} %param.20) | copy-start | bytes 786436
  0.7 22.1 %copy-start.10 = (bf16[256]{0:T(256)(128)(2,1)S(1)}, bf16[256]{0:T(256)(128)(2,1)}, u32[]{:S(2)}) copy-start(bf16[256]{0:T(256)(128)(2,1)} %param.29) | copy-start | bytes 1540
  2.2 20.6 %collective-permute-start = (bf16[3,1536]{1,0:T(4,128)(2,1)S(1)}, bf16[3,1536]{1,0:T(4,128)(2,1)S(1)}, u32[]{:S(2)}, u32[]{:S(2)}) collective-permute-start(bf16[3,1536]{1,0:T(4,128)(2,1)S(1)} %pad_maximum_fusion.4), channel_id=1, source_target_pairs={{0,4},{4,8},{8,12},{1,5},{5,9},{9,13},{2,6},{6,10},{10,14},{3,7},{... | collective-permute-start | bytes 27656 | tf_op jit(solution)/shard_map/ppermute | solution.py:28
  24.5 15.9 %copy-start.7 = (bf16[1280]{0:T(1024)(128)(2,1)S(1)}, bf16[1280]{0:T(1024)(128)(2,1)}, u32[]{:S(2)}) copy-start(bf16[1280]{0:T(1024)(128)(2,1)} %param.30) | copy-start | bytes 7684
  36.7 18.9 %collective-permute-start.1 = (f32[20,72,128]{2,1,0:T(8,128)S(1)}, f32[20,72,128]{2,1,0:T(8,128)S(1)}, u32[]{:S(2)}, u32[]{:S(2)}) collective-permute-start(f32[20,72,128]{2,1,0:T(8,128)S(1)} %pad_maximum_fusion), channel_id=1, source_target_pairs={{0,4},{4,8},{8,12},{1,5},{5,9},{9,13},{2,6},{6,10},{10,14},{3,7},{... | collective-permute-start | bytes 2211848 | tf_op jit(solution)/shard_map/ppermute | solution.py:28
  55.7 19.0 %collective-permute-start.2 = (f32[20,72,128]{2,1,0:T(8,128)S(1)}, f32[20,72,128]{2,1,0:T(8,128)S(1)}, u32[]{:S(2)}, u32[]{:S(2)}) collective-permute-start(f32[20,72,128]{2,1,0:T(8,128)S(1)} %collective-permute-done.1), channel_id=1, source_target_pairs={{0,4},{4,8},{8,12},{1,5},{5,9},{9,13},{2,6},{6,10},{10,14},{3,7},{... | collective-permute-start | bytes 2211848 | tf_op jit(solution)/shard_map/ppermute | solution.py:28
  74.8 19.2 %collective-permute-start.3 = (f32[20,72,128]{2,1,0:T(8,128)S(1)}, f32[20,72,128]{2,1,0:T(8,128)S(1)}, u32[]{:S(2)}, u32[]{:S(2)}) collective-permute-start(f32[20,72,128]{2,1,0:T(8,128)S(1)} %pad_maximum_fusion.1), channel_id=1, source_target_pairs={{0,8},{4,12},{1,9},{5,13},{2,10},{6,14},{3,11},{7,15},{16,24},{20,... | collective-permute-start | bytes 2211848 | tf_op jit(solution)/shard_map/ppermute | solution.py:28
  95.0 1.7 copy-start.2
  95.0 2.1 copy-start.4
  109.6 92.2 %collective-permute-start.4 = (f32[512,1280]{1,0:T(8,128)}, f32[512,1280]{1,0:T(8,128)}, u32[]{:S(2)}, u32[]{:S(2)}) collective-permute-start(f32[512,1280]{1,0:T(8,128)} %fusion.3), channel_id=1, source_target_pairs={{0,1},{1,0},{2,3},{3,2},{4,5},{5,4},{6,7},{7,6},{8,9},{9,8},{10,11... | collective-permute-start | bytes 7864328 | tf_op jit(solution)/shard_map/ppermute | solution.py:38
  109.6 44.7 %collective-permute-start.6 = (bf16[320,1664]{1,0:T(8,128)(2,1)}, bf16[320,1664]{1,0:T(8,128)(2,1)}, u32[]{:S(2)}, u32[]{:S(2)}) collective-permute-start(bf16[320,1664]{1,0:T(8,128)(2,1)} %get-tuple-element.24), channel_id=1, source_target_pairs={{0,4},{4,8},{8,12},{12,0},{1,5},{5,9},{9,13},{13,1},{2,6},{6,10},{... | collective-permute-start | bytes 3194888 | tf_op jit(solution)/shard_map/ppermute | solution.py:33
  126.7 73.0 %collective-permute-start.8 = (bf16[320,1664]{1,0:T(8,128)(2,1)}, bf16[320,1664]{1,0:T(8,128)(2,1)}, u32[]{:S(2)}, u32[]{:S(2)}) collective-permute-start(bf16[320,1664]{1,0:T(8,128)(2,1)} %get-tuple-element.10), channel_id=1, source_target_pairs={{0,8},{4,12},{8,0},{12,4},{1,9},{5,13},{9,1},{13,5},{2,10},{6,14},... | collective-permute-start | bytes 3194888 | tf_op jit(solution)/shard_map/ppermute | solution.py:33
  130.1 71.2 %collective-permute-start.10 = (bf16[320,1664]{1,0:T(8,128)(2,1)}, bf16[320,1664]{1,0:T(8,128)(2,1)}, u32[]{:S(2)}, u32[]{:S(2)}) collective-permute-start(bf16[320,1664]{1,0:T(8,128)(2,1)} %get-tuple-element.11), channel_id=1, source_target_pairs={{0,12},{4,0},{8,4},{12,8},{1,13},{5,1},{9,5},{13,9},{2,14},{6,2},{... | collective-permute-start | bytes 3194888 | tf_op jit(solution)/shard_map/ppermute | solution.py:33
  154.3 55.8 %collective-permute-start.7 = (bf16[320,1664]{1,0:T(8,128)(2,1)}, bf16[320,1664]{1,0:T(8,128)(2,1)}, u32[]{:S(2)}, u32[]{:S(2)}) collective-permute-start(bf16[320,1664]{1,0:T(8,128)(2,1)} %collective-permute-done.6), channel_id=1, source_target_pairs={{0,16},{16,0},{1,17},{17,1},{2,18},{18,2},{3,19},{19,3},{4,20},{20... | collective-permute-start | bytes 3194888 | tf_op jit(solution)/shard_map/ppermute | solution.py:33
  199.7 26.6 %collective-permute-start.9 = (bf16[320,1664]{1,0:T(8,128)(2,1)}, bf16[320,1664]{1,0:T(8,128)(2,1)S(1)}, u32[]{:S(2)}, u32[]{:S(2)}) collective-permute-start(bf16[320,1664]{1,0:T(8,128)(2,1)} %collective-permute-done.8), channel_id=1, source_target_pairs={{0,16},{16,0},{1,17},{17,1},{2,18},{18,2},{3,19},{19,3},{4,20},{20... | collective-permute-start | bytes 3194888 | tf_op jit(solution)/shard_map/ppermute | solution.py:33
  201.3 46.9 %collective-permute-start.11 = (bf16[320,1664]{1,0:T(8,128)(2,1)}, bf16[320,1664]{1,0:T(8,128)(2,1)S(1)}, u32[]{:S(2)}, u32[]{:S(2)}) collective-permute-start(bf16[320,1664]{1,0:T(8,128)(2,1)} %collective-permute-done.10), channel_id=1, source_target_pairs={{0,16},{16,0},{1,17},{17,1},{2,18},{18,2},{3,19},{19,3},{4,20},{20... | collective-permute-start | bytes 3194888 | tf_op jit(solution)/shard_map/ppermute | solution.py:33
  206.6 42.7 %collective-permute-start.5 = (f32[512,640]{1,0:T(8,128)S(1)}, f32[512,640]{1,0:T(8,128)S(1)}, u32[]{:S(2)}, u32[]{:S(2)}) collective-permute-start(f32[512,640]{1,0:T(8,128)S(1)} %slice.130), channel_id=1, source_target_pairs={{0,2},{1,3},{2,0},{3,1},{4,6},{5,7},{6,4},{7,5},{8,10},{9,11},{10,... | collective-permute-start | bytes 3932168 | tf_op jit(solution)/shard_map/ppermute | solution.py:33
  227.4 21.9 %copy-start.5 = (bf16[512,640]{1,0:T(8,128)(2,1)S(1)}, bf16[512,640]{1,0:T(8,128)(2,1)}, u32[]{:S(2)}) copy-start(bf16[512,640]{1,0:T(8,128)(2,1)} %param.18) | copy-start | bytes 1966084
  249.3 7.2 %copy-start.8 = (s32[512]{0:T(512)S(1)}, s32[512]{0:T(512)}, u32[]{:S(2)}) copy-start(s32[512]{0:T(512)} %param.34) | copy-start | bytes 6148
  249.7 109.2 %copy-start.3 = (bf16[512,640]{1,0:T(8,128)(2,1)}, bf16[512,640]{1,0:T(8,128)(2,1)S(1)}, u32[]{:S(2)}) copy-start(bf16[512,640]{1,0:T(8,128)(2,1)S(1)} %get-tuple-element.17) | copy-start | bytes 1966084
  257.1 102.5 %copy-start.9 = (s32[4]{0:T(128)S(1)}, s32[4]{0:T(128)}, u32[]{:S(2)}) copy-start(s32[4]{0:T(128)} %param.35) | copy-start | bytes 52
  257.1 103.1 %copy-start.1 = (f32[20]{0:T(128)S(1)}, f32[20]{0:T(128)}, u32[]{:S(2)}) copy-start(f32[20]{0:T(128)} %param.25) | copy-start | bytes 244
where the time goes:
time: 361 us; the launch traced here: 360 us
  Pallas kernels  125 us (35%)
  waiting for transfers between devices  107 us (30%)
  starting transfers between devices  43.7 us (12%)
  local copies, waits for them, and re-layouts  42 us (12%)
  other arithmetic  15.2 us (4%)
  matrix products  14.3 us (4%)
  blocking collectives  11.5 us (3%)
    pallas_call x1, Pallas kernels, loss_stage(): pl.pallas_call(functools.partial(tail_kernel, n, heads, first_of), out_sh...  102 us
    ppermute x7, waiting for transfers between devices, rotated(): lax.ppermute(array, axis, [(i, (i + by) % length) for i in range(length)])  88.9 us
    ppermute x7, starting transfers between devices, rotated(): lax.ppermute(array, axis, [(i, (i + by) % length) for i in range(length)])  25.3 us
    ppermute x4, starting transfers between devices, shifted(): return lax.ppermute(array, axis, pairs)  18.4 us
    ppermute x4, waiting for transfers between devices, shifted(): return lax.ppermute(array, axis, pairs)  18 us
    pallas_call x1, Pallas kernels, within(): pl.pallas_call(within_kernel, grid=(inner_here // lanes,), in_specs=[pl.B...  12 us
    dynamic_update_slice x6, local copies, waits for them, and re-layouts, local(): lax.dynamic_update_slice_in_dim(vocab_weight, bands[by - 1][hop], start, 0)  11.5 us
    pallas_call x1, Pallas kernels, conv_state(): pl.pallas_call(conv_state_kernel, grid=(inner_here // lanes,), in_specs=[...  11 us
  transfers between devices with their start and end apart: 12, of which 7 were waited for; matrix products, arithmetic and copies ran while one was open for 15% of the time, Pallas kernels for 3%

commit v1 on v0

--- a/solution.py
+++ b/solution.py
@@ -97,10 +97,6 @@
         )
         reach *= 2
     return packed[:, :extent]
-
-
-def share_of(array):
-    return array.shape[1] % TILE == 0
 
 
 def document_of(positions, doc_lengths):
@@ -220,31 +216,61 @@
     )(values, scores, cols, rows, skip)
 
 
-TAIL_ROWS = 256
 TILE = 128
-
-
-def tail_kernel(
-    n, heads, first_of, hid_ref, tgt_ref, member_ref, w_ref, out_ref,
-    full, w_buf, tgts, marks, parts, sums,
-    w_sem, along_send, side_send, arrive, tgt_send, tgt_recv, mark_send, mark_recv, sum_send, sum_recv,
+LOSS_ROWS = 256
+HALO = 16
+PARTS = 2
+
+
+def block_kernel(
+    n, heads, groups, inner, features,
+    x_ref, z_ref, bc_ref, taps_ref, bias_ref, bc_taps_ref, bc_bias_ref, cols_ref, rows_ref,
+    same_ref, doc_ref, skip_ref, gain_ref, res_ref, final_ref, tgt_ref, member_ref, ow_ref, lm_ref,
+    block_ref, out_ref,
+    ow_buf, w_buf, full, tgts, marks, parts, sums, halo_x, halo_bc, held, masks, values, keys,
+    scores, state_out, state_in, gated, squares, tiles, normed, share_out, share_in, hid,
+    load_sem, halo_send, halo_recv, w_send, w_recv, y_send, y_recv, state_send, state_recv,
+    tile_send, tile_recv, share_send, share_recv,
+    along_send, side_send, arrive, tgt_send, tgt_recv, mark_send, mark_recv, sum_send, sum_recv,
 ):
+    g = lax.axis_index("groups")
     z = lax.axis_index("seq")
     h = lax.axis_index("head")
-    rows, share = hid_ref.shape
-    width = w_ref.shape[1]
+    length, inner_here = x_ref.shape
+    share = res_ref.shape[1]
+    depth, columns = lm_ref.shape
+    width = w_buf.shape[1]
+    band = depth // groups
+    sub = band // PARTS
     total_peers = n * heads
     me = z * heads + h
     twin = h + 1 - 2 * lax.rem(h, 2)
     side = lax.rem(h + 2, heads)
-
-    load = pltpu.make_async_copy(w_ref, w_buf, w_sem)
-    load.start()
-    barrier = pltpu.get_barrier_semaphore()
+    chunks = inner_here // TILE
+
+    def remote(src, dst, send, recv, target):
+        return pltpu.make_async_remote_copy(
+            src_ref=src, dst_ref=dst, send_sem=send, recv_sem=recv,
+            device_id=target, device_id_type=MESH,
+        )
+
+    def window(rank):
+        return pl.multiple_of(rank * width - rank // (n - 1) * (n * width - columns), TILE)
 
     def peer(k):
         flat = lax.rem(me + k, total_peers)
         return flat // heads, lax.rem(flat, heads)
+
+    load_out = pltpu.make_async_copy(ow_ref, ow_buf, load_sem.at[0])
+    load_own = pltpu.make_async_copy(
+        lm_ref.at[:, pl.ds(window(z), width)],
+        w_buf.at[pl.ds(pl.multiple_of(z * depth, 16), depth), :],
+        load_sem.at[1],
+    )
+    load_out.start()
+    load_own.start()
+
+    barrier = pltpu.get_barrier_semaphore()
 
     @pl.loop(1, total_peers)
     def _(k):
@@ -253,86 +279,330 @@
             barrier, inc=1, device_id={"seq": there, "head": where_head}, device_id_type=MESH
         )
 
-    pl.semaphore_wait(barrier, total_peers - 1)
+    for hop in range(1, groups):
+        pl.semaphore_signal(
+            barrier, inc=1, device_id={"groups": lax.rem(g + hop, groups)}, device_id_type=MESH
+        )
+    pl.semaphore_wait(barrier, total_peers - 1 + groups - 1)
+
+    def halo_copies():
+        tail_rows = pl.ds(length - HALO, HALO)
+        return [
+            remote(x_ref.at[tail_rows, :], halo_x, halo_send.at[0], halo_recv.at[0], {"seq": z + 1}),
+            remote(bc_ref.at[tail_rows, :], halo_bc, halo_send.at[1], halo_recv.at[1], {"seq": z + 1}),
+        ]
+
+    @pl.when(z < n - 1)
+    def _():
+        for copy in halo_copies():
+            copy.start()
+
+    def w_rows(source, group, part):
+        return pl.ds(pl.multiple_of(source * depth + group * band + part * sub, 16), sub)
+
+    def w_copy(k, part):
+        there = lax.rem(z + k, n)
+        return remote(
+            lm_ref.at[pl.ds(pl.multiple_of(g * band + part * sub, 16), sub), pl.ds(window(there), width)],
+            w_buf.at[w_rows(z, g, part), :],
+            w_send.at[k, part],
+            w_recv.at[z, part],
+            {"seq": there},
+        )
+
+    def w_forward(source, part, hop):
+        place = w_buf.at[w_rows(source, g, part), :]
+        return remote(
+            place, place, y_send.at[source, part, hop], y_recv.at[g, source, part],
+            {"groups": lax.rem(g + hop, groups)},
+        )
+
+    def w_pass_on(k, part):
+        source = lax.rem(z + n - k, n)
+        place = w_buf.at[w_rows(source, g, part), :]
+        remote(place, place, w_send.at[k, part], w_recv.at[source, part], {"seq": source}).wait_recv()
+        for hop in range(1, groups):
+            w_forward(source, part, hop).start()
+
+    def w_start(k):
+        for part in range(PARTS):
+            w_copy(k, part).start()
+
+    w_start(1)
+    for k in range(2, n):
+        @pl.when(z + k >= n)
+        def _():
+            w_start(k)
+
+    def tell(k, source):
+        return remote(
+            tgt_ref, tgts.at[source], tgt_send.at[k], tgt_recv.at[source],
+            {"seq": lax.rem(z + k, n)},
+        )
+
+    for k in range(1, n):
+        tell(k, z).start()
+    tgts[z] = tgt_ref[...]
+
+    for lag in range(1, KERNEL):
+        masks[lag - 1] = jnp.broadcast_to(same_ref[:, lag : lag + 1], (length, TILE))
+
+    @pl.when(z == 0)
+    def _():
+        halo_x[...] = jnp.zeros_like(halo_x)
+        halo_bc[...] = jnp.zeros_like(halo_bc)
+        state_in[...] = jnp.zeros_like(state_in)
+
+    @pl.when(z > 0)
+    def _():
+        for copy in halo_copies():
+            copy.wait_recv()
+
+    def convolved(signal, halo, weight, bias, lanes):
+        held[0:HALO, :] = halo[:, lanes].astype(jnp.float32)
+        held[HALO:, :] = signal[:, lanes].astype(jnp.float32)
+        total = jnp.zeros((length, TILE), jnp.float32) + bias[:, lanes]
+        for offset in range(KERNEL):
+            lag = KERNEL - 1 - offset
+            term = weight[offset : offset + 1, lanes] * held[HALO - lag : HALO - lag + length, :]
+            total = total + (term * masks[lag - 1] if lag else term)
+        return jax.nn.silu(total).astype(jnp.bfloat16)
+
+    for half in range(2):
+        lanes = pl.ds(half * STATE, STATE)
+        keys[:, lanes] = convolved(bc_ref, halo_bc, bc_taps_ref, bc_bias_ref, lanes)
+    nt = (((1,), (1,)), ((), ()))
+    for cut in range(0, length, SPAN):
+        near = pl.ds(cut, SPAN)
+        inside = (same_ref[near, 5:6] == doc_ref[0:1, :]) & (
+            lax.broadcasted_iota(jnp.int32, (SPAN, length), 0) + cut
+            >= lax.broadcasted_iota(jnp.int32, (SPAN, length), 1)
+        )
+        product = lax.dot_general(
+            keys[near, STATE:], keys[:, :STATE], nt, preferred_element_type=jnp.float32
+        )
+        scores[near, :] = jnp.where(inside, product, 0.0)
+
+    def state_copy(c):
+        return remote(
+            state_out.at[c], state_in.at[c], state_send.at[c], state_recv.at[c], {"seq": z + 1}
+        )
+
+    first = lax.broadcasted_iota(jnp.int32, (SPAN, TILE), 1) < HEAD_SIZE
+
+    @pl.loop(0, chunks)
+    def _(c):
+        lanes = pl.ds(pl.multiple_of(c * TILE, TILE), TILE)
+        own = convolved(x_ref, halo_x, taps_ref, bias_ref, lanes)
+        values[:, lanes] = own
+        early = lax.broadcasted_iota(jnp.int32, (length, TILE), 1) < HEAD_SIZE
+        decay = jnp.where(early, cols_ref[c, :, 2:3], cols_ref[c, :, 3:4])
+        scaled = own.astype(jnp.float32) * decay
+        high = scaled.astype(jnp.bfloat16)
+        low = (scaled - high.astype(jnp.float32)).astype(jnp.bfloat16)
+        bmat = keys[:, :STATE]
+        tn = (((0,), (0,)), ((), ()))
+        state_out[c] = lax.dot_general(
+            high, bmat, tn, preferred_element_type=jnp.float32
+        ) + lax.dot_general(low, bmat, tn, preferred_element_type=jnp.float32)
+
+        @pl.when(z == 0)
+        def _():
+            state_copy(c).start()
+
+    squares[...] = jnp.zeros_like(squares)
+
+    @pl.loop(0, chunks)
+    def _(c):
+        lanes = pl.ds(pl.multiple_of(c * TILE, TILE), TILE)
+
+        @pl.when(z > 0)
+        def _():
+            state_copy(c).wait_recv()
+
+        @pl.when((z > 0) & (z < n - 1))
+        def _():
+            top = lax.broadcasted_iota(jnp.int32, (TILE, STATE), 0) < HEAD_SIZE
+            final = cols_ref[c, length - 1 : length, 0:2]
+            through = jnp.where(top, jnp.exp(-final[:, 0:1]), jnp.exp(-final[:, 1:2]))
+            through = through * same_ref[length - 1 : length, 4:5]
+            state_out[c] = through * state_in[c] + state_out[c]
+            state_copy(c).start()
+
+        incoming = state_in[c]
+        in_high = incoming.astype(jnp.bfloat16)
+        in_low = (incoming - in_high.astype(jnp.float32)).astype(jnp.bfloat16)
+        for cut in range(0, length, SPAN):
+            upto = cut + SPAN
+            near = pl.ds(cut, SPAN)
+            signal = values[0:upto, lanes]
+            sums_of = []
+            entries = []
+            for which in range(2):
+                climb = cols_ref[c, near, which : which + 1]
+                gap = rows_ref[c, which : which + 1, 0:upto] - climb
+                weights = (
+                    jnp.exp(jnp.minimum(gap, 0.0))
+                    * scores[near, 0:upto]
+                    * rows_ref[c, 2 + which : 3 + which, 0:upto]
+                )
+                high = weights.astype(jnp.bfloat16)
+                low = (weights - high.astype(jnp.float32)).astype(jnp.bfloat16)
+                sums_of.append(
+                    jnp.dot(high, signal, preferred_element_type=jnp.float32)
+                    + jnp.dot(low, signal, preferred_element_type=jnp.float32)
+                )
+                entries.append(jnp.exp(-climb) * same_ref[near, 4:5])
+            cmat = keys[near, STATE:]
+            arriving = lax.dot_general(
+                cmat, in_high, nt, preferred_element_type=jnp.float32
+            ) + lax.dot_general(cmat, in_low, nt, preferred_element_type=jnp.float32)
+            mixed = (
+                jnp.where(first, sums_of[0], sums_of[1])
+                + skip_ref[:, lanes] * values[near, lanes].astype(jnp.float32)
+                + arriving * jnp.where(first, entries[0], entries[1])
+            )
+            result = mixed * jax.nn.silu(z_ref[near, lanes].astype(jnp.float32))
+            gated[near, lanes] = result
+            squares[near, :] += result * result
+
+    for k in range(2, n):
+        @pl.when(z + k < n)
+        def _():
+            w_start(k)
+
+    def tile_copy(which, k, slot_of):
+        return remote(
+            tiles.at[which, slot_of], tiles.at[which, slot_of], tile_send.at[which, k],
+            tile_recv.at[which, slot_of], {"head": lax.rem(h + k, heads)},
+        )
+
+    def scale_of(which, partial, count):
+        column = jnp.broadcast_to(jnp.sum(partial, axis=1, keepdims=True), (length, TILE))
+        tiles[which, h] = jnp.transpose(column)[0:8, :]
+        for k in range(1, heads):
+            tile_copy(which, k, h).start()
+        for k in range(1, heads):
+            tile_copy(which, k, lax.rem(h + k, heads)).wait()
+        total = tiles[which, 0]
+        for head in range(1, heads):
+            total = total + tiles[which, head]
+        scale = lax.rsqrt(total / count + EPSILON)
+        return jnp.transpose(jnp.broadcast_to(scale[0:1, :], (TILE, length)))
+
+    squares[...] = scale_of(0, squares[...], inner)
+
+    @pl.loop(0, chunks)
+    def _(c):
+        lanes = pl.ds(pl.multiple_of(c * TILE, TILE), TILE)
+        normed[:, lanes] = (gated[:, lanes] * squares[...] * gain_ref[:, lanes]).astype(jnp.bfloat16)
+
+    load_out.wait()
+
+    def project(head, slot_of):
+        @pl.loop(0, length // LOSS_ROWS)
+        def _(step):
+            near = pl.ds(pl.multiple_of(step * LOSS_ROWS, LOSS_ROWS), LOSS_ROWS)
+            share_out[slot_of, near, :] = jnp.dot(
+                normed[near, :],
+                ow_buf[:, pl.ds(pl.multiple_of(head * share, TILE), share)],
+                preferred_element_type=jnp.float32,
+            )
+
+    def share_copy(slot_of, target):
+        return remote(
+            share_out.at[slot_of], share_in.at[slot_of], share_send.at[slot_of],
+            share_recv.at[slot_of], {"head": target},
+        )
+
+    project(lax.rem(twin + 2, heads), 0)
+    share_copy(0, twin).start()
+    project(side, 1)
+    share_copy(0, twin).wait_recv()
+    share_out[1] = share_out[1] + share_in[0]
+    share_copy(1, side).start()
+    project(twin, 2)
+    share_copy(2, twin).start()
+    for part in range(PARTS):
+        w_pass_on(1, part)
+    project(h, 3)
+    share_copy(2, twin).wait_recv()
+    share_copy(1, side).wait_recv()
+
+    @pl.loop(0, length // LOSS_ROWS)
+    def _(step):
+        near = pl.ds(pl.multiple_of(step * LOSS_ROWS, LOSS_ROWS), LOSS_ROWS)
+        total = share_out[3, near, :] + share_in[2, near, :] + share_in[1, near, :]
+        block_ref[near, :] = (res_ref[near, :].astype(jnp.float32) + total).astype(jnp.bfloat16)
+
+    square = jnp.zeros((length, TILE), jnp.float32)
+    for cut in range(0, share, TILE):
+        piece = block_ref[:, cut : cut + TILE].astype(jnp.float32)
+        square = square + piece * piece
+    squares[...] = scale_of(1, square, features)
+    for cut in range(0, share, TILE):
+        piece = block_ref[:, cut : cut + TILE].astype(jnp.float32)
+        hid[:, cut : cut + TILE] = (
+            piece * squares[...] * final_ref[:, cut : cut + TILE]
+        ).astype(jnp.bfloat16)
+
+    full[z, :, pl.ds(pl.multiple_of(h * share, TILE), share)] = hid[...]
 
     def slot(block, head):
         return full.at[block, :, pl.ds(pl.multiple_of(head * share, TILE), share)]
 
-    def ship(kind, block, head, target, source=None):
-        sem = along_send if kind < 2 else side_send
-        return pltpu.make_async_remote_copy(
-            src_ref=slot(block, head) if source is None else source,
-            dst_ref=slot(block, head),
-            send_sem=sem.at[kind % 2, block, head] if kind < 2 else sem.at[kind - 2, block, head],
-            recv_sem=arrive.at[block, head],
-            device_id=target,
-            device_id_type=MESH,
+    def ship(sem, block, head, target, source=None):
+        return remote(
+            slot(block, head) if source is None else source, slot(block, head),
+            sem, arrive.at[block, head], target,
         )
 
     def right(block, source=None):
-        return ship(0, block, h, {"seq": z + 1}, source)
+        return ship(along_send.at[0, block], block, h, {"seq": z + 1}, source)
 
     def left(block, source=None):
-        return ship(1, block, h, {"seq": z - 1}, source)
+        return ship(along_send.at[1, block], block, h, {"seq": z - 1}, source)
 
     def across(block, source=None):
-        return ship(2, block, h, {"head": side}, source)
-
-    def twinned(block, head, source=None):
-        return ship(3, block, head, {"head": twin}, source)
+        return ship(side_send.at[block], block, h, {"head": side}, source)
+
+    def twinned(kind, block, head, source=None):
+        return ship(along_send.at[2 + kind, block], block, head, {"head": twin}, source)
 
     def arrived(block, head):
-        ship(0, block, head, {"head": twin}).wait_recv()
-
-    def tell(k):
-        return pltpu.make_async_remote_copy(
-            src_ref=tgt_ref,
-            dst_ref=tgts.at[z],
-            send_sem=tgt_send.at[k],
-            recv_sem=tgt_recv.at[z],
-            device_id={"seq": lax.rem(z + k, n)},
-            device_id_type=MESH,
-        )
-
-    across(z, hid_ref).start()
+        twinned(0, block, head).wait_recv()
+
+    across(z, hid).start()
 
     @pl.when(z < n - 1)
     def _():
-        right(z, hid_ref).start()
+        right(z, hid).start()
 
     @pl.when(z > 0)
     def _():
-        left(z, hid_ref).start()
-
-    twinned(z, h, hid_ref).start()
-    for k in range(1, n):
-        tell(k).start()
-    tgts[z] = tgt_ref[...]
-    full[z, :, pl.ds(pl.multiple_of(h * share, TILE), share)] = hid_ref[...]
-    load.wait()
+        left(z, hid).start()
+
+    twinned(0, z, h, hid).start()
 
     def mark_copy(block, head):
-        return pltpu.make_async_remote_copy(
-            src_ref=marks.at[block, :, pl.ds(pl.multiple_of(head * TILE, TILE), TILE)],
-            dst_ref=parts.at[me],
-            send_sem=mark_send.at[block, head],
-            recv_sem=mark_recv.at[me],
-            device_id={"seq": block, "head": head},
-            device_id_type=MESH,
-        )
+        return remote(
+            marks.at[block, :, pl.ds(pl.multiple_of(head * TILE, TILE), TILE)], parts.at[me],
+            mark_send.at[block, head], mark_recv.at[me], {"seq": block, "head": head},
+        )
+
+    dead = z * width - window(z)
+    start_column = h * columns + window(z)
 
     def compute(block):
-        dead, first = first_of(z, h, width)
-
-        @pl.loop(0, rows // TAIL_ROWS)
+        @pl.loop(0, length // LOSS_ROWS)
         def _(step):
-            at = pl.multiple_of(step * TAIL_ROWS, TAIL_ROWS)
+            at = pl.multiple_of(step * LOSS_ROWS, LOSS_ROWS)
             logits = jnp.dot(
-                full[block, pl.ds(at, TAIL_ROWS), :], w_buf[...], preferred_element_type=jnp.float32
+                full[block, pl.ds(at, LOSS_ROWS), :], w_buf[...], preferred_element_type=jnp.float32
             )
-            wanted = tgts[block, 0:1, pl.ds(at, TAIL_ROWS)]
-            wanted = jnp.transpose(jnp.broadcast_to(wanted, (TILE, TAIL_ROWS))) - first
-            lane = lax.broadcasted_iota(jnp.int32, (TAIL_ROWS, TILE), 1)
+            wanted = tgts[block, 0:1, pl.ds(at, LOSS_ROWS)]
+            wanted = jnp.transpose(jnp.broadcast_to(wanted, (TILE, LOSS_ROWS))) - start_column
+            lane = lax.broadcasted_iota(jnp.int32, (LOSS_ROWS, TILE), 1)
             pieces = []
             for cut in range(0, width, TILE):
                 piece = logits[:, cut : cut + TILE]
@@ -341,8 +611,8 @@
             for piece in pieces[1:]:
                 peak = jnp.maximum(peak, piece)
             peak = jnp.max(peak, axis=1, keepdims=True)
-            total = jnp.zeros((TAIL_ROWS, TILE), jnp.float32)
-            picked = jnp.zeros((TAIL_ROWS, TILE), jnp.float32)
+            total = jnp.zeros((LOSS_ROWS, TILE), jnp.float32)
+            picked = jnp.zeros((LOSS_ROWS, TILE), jnp.float32)
             for index, piece in enumerate(pieces):
                 total = total + jnp.exp(piece - peak)
                 here = (lane + index * TILE == wanted) & (lane + index * TILE >= dead)
@@ -350,7 +620,7 @@
             total = jnp.sum(total, axis=1, keepdims=True)
             picked = jnp.sum(picked, axis=1, keepdims=True)
             tile = jnp.where(lane == 0, peak, jnp.where(lane == 1, total, picked))
-            marks[block, :, pl.ds(at, TAIL_ROWS)] = jnp.transpose(tile)[0:8, :]
+            marks[block, :, pl.ds(at, LOSS_ROWS)] = jnp.transpose(tile)[0:8, :]
 
         @pl.loop(0, heads)
         def _(head):
@@ -360,10 +630,14 @@
 
     def finish(block):
         arrived(block, side)
-        twinned(block, side).start()
+        twinned(1, block, side).start()
         arrived(block, twin)
         arrived(block, lax.rem(twin + 2, heads))
         compute(block)
+
+    for k in range(2, n):
+        for part in range(PARTS):
+            w_pass_on(k, part)
 
     for step in range(1, n):
         @pl.when(z >= step)
@@ -376,7 +650,7 @@
                 right(block).start()
 
             across(block).start()
-            twinned(block, h).start()
+            twinned(0, block, h).start()
 
         @pl.when(z + step < n)
         def _():
@@ -388,19 +662,21 @@
                 left(block).start()
 
             across(block).start()
-            twinned(block, h).start()
+            twinned(0, block, h).start()
 
         if step == 1:
+            load_own.wait()
             for k in range(1, n):
                 source = lax.rem(z + n - k, n)
-                pltpu.make_async_remote_copy(
-                    src_ref=tgt_ref,
-                    dst_ref=tgts.at[source],
-                    send_sem=tgt_send.at[k],
-                    recv_sem=tgt_recv.at[source],
-                    device_id={"seq": lax.rem(z + k, n)},
-                    device_id_type=MESH,
-                ).wait()
+                tell(k, source).wait()
+                for hop in range(1, groups):
+                    other = lax.rem(g + groups - hop, groups)
+                    for part in range(PARTS):
+                        place = w_buf.at[w_rows(source, other, part), :]
+                        remote(
+                            place, place, y_send.at[source, part, hop],
+                            y_recv.at[other, source, part], {"groups": other},
+                        ).wait_recv()
             finish(z)
         else:
             @pl.when(z >= step - 1)
@@ -411,32 +687,54 @@
             def _():
                 finish(z + step - 1)
 
-    if n > 1:
-        @pl.when(z >= n - 1)
+    @pl.when(z >= n - 1)
+    def _():
+        finish(z - n + 1)
+
+    @pl.when(z + n - 1 < n)
+    def _():
+        finish(z + n - 1)
+
+    @pl.when(z < n - 1)
+    def _():
+        for copy in halo_copies():
+            copy.wait_send()
+
+        @pl.loop(0, chunks)
+        def _(c):
+            state_copy(c).wait_send()
+
+    for slot_of, target in ((0, twin), (1, side), (2, twin)):
+        share_copy(slot_of, target).wait_send()
+    for k in range(1, n):
+        source = lax.rem(z + n - k, n)
+        for part in range(PARTS):
+            w_copy(k, part).wait_send()
+            for hop in range(1, groups):
+                w_forward(source, part, hop).wait_send()
+    for block in range(n):
+        @pl.when((z < n - 1) & (z >= block))
         def _():
-            finish(z - n + 1)
-
-        @pl.when(z + n - 1 < n)
+            right(block).wait_send()
+
+        @pl.when((z > 0) & (z <= block))
         def _():
-            finish(z + n - 1)
+            left(block).wait_send()
+
+        across(block).wait_send()
+        twinned(0, block, h).wait_send()
+        twinned(1, block, side).wait_send()
 
     parts[me] = marks[z, :, pl.ds(pl.multiple_of(h * TILE, TILE), TILE)]
 
-    def mark_arrival(k):
+    @pl.loop(1, total_peers)
+    def _(k):
         there, where_head = peer(k)
         flat = there * heads + where_head
-        pltpu.make_async_remote_copy(
-            src_ref=parts.at[flat],
-            dst_ref=parts.at[flat],
-            send_sem=mark_send.at[there, where_head],
-            recv_sem=mark_recv.at[flat],
-            device_id={"seq": there, "head": where_head},
-            device_id_type=MESH,
+        remote(
+            parts.at[flat], parts.at[flat], mark_send.at[there, where_head], mark_recv.at[flat],
+            {"seq": there, "head": where_head},
         ).wait()
-
-    @pl.loop(1, total_peers)
-    def _(k):
-        mark_arrival(k)
 
     peak = parts[0, 0:1, :]
     for flat in range(1, total_peers):
@@ -452,31 +750,14 @@
 
     def sum_copy(k, slot_of):
         there, where_head = peer(k)
-        return pltpu.make_async_remote_copy(
-            src_ref=sums.at[slot_of],
-            dst_ref=sums.at[slot_of],
-            send_sem=sum_send.at[k],
-            recv_sem=sum_recv.at[slot_of],
-            device_id={"seq": there, "head": where_head},
-            device_id_type=MESH,
+        return remote(
+            sums.at[slot_of], sums.at[slot_of], sum_send.at[k], sum_recv.at[slot_of],
+            {"seq": there, "head": where_head},
         )
 
     @pl.loop(1, total_peers)
     def _(k):
         sum_copy(k, me).start()
-
-    for block in range(n):
-        @pl.when((z < n - 1) & (z >= block))
-        def _():
-            right(block).wait_send()
-
-        @pl.when((z > 0) & (z <= block))
-        def _():
-            left(block).wait_send()
-
-        across(block).wait_send()
-        twinned(block, h).wait_send()
-        twinned(block, side).wait_send()
 
     @pl.loop(1, total_peers)
     def _(k):
@@ -488,27 +769,74 @@
     out_ref[...] = grand
 
 
-def loss_stage(hidden_part, targets_row, member, weight, n, heads, first_of):
-    rows, _ = hidden_part.shape
-    deep, width = weight.shape
+def fits(length, inner_here, share, depth, columns, width, n, heads, groups):
+    room = 2 * (n * length * n * depth + n * depth * width + inner_here * n * depth)
+    room += 4 * (length * inner_here * 4 + 6 * length * share + length * length)
+    even = [inner_here % TILE, share % TILE, columns % TILE, depth % (groups * PARTS * 16)]
+    even += [length % SPAN, length % LOSS_ROWS, length - heads * TILE, heads - 4]
+    even += [share * heads - depth * n]
+    return not any(even) and n > 1 and (n - 1) * width <= columns and room < 56 * 2**20
+
+
+def block_stage(operands, whole, member, width, n, heads, groups):
+    x_in, res = operands[0], operands[13]
+    out_weight, _ = whole
+    length, inner_here = x_in.shape
+    share = res.shape[1]
+    features = out_weight.shape[1]
     peers = n * heads
+    chunks = inner_here // TILE
     dma = pltpu.SemaphoreType.DMA
-    flops = 2 * n * rows * deep * width
+    vmem = pltpu.VMEM
+    f32, bf16 = jnp.float32, jnp.bfloat16
     return pl.pallas_call(
-        functools.partial(tail_kernel, n, heads, first_of),
-        out_shape=jax.ShapeDtypeStruct(member.shape, jnp.float32),
-        in_specs=[pl.BlockSpec(memory_space=pltpu.VMEM)] * 3 + [pl.BlockSpec(memory_space=pl.ANY)],
-        out_specs=pl.BlockSpec(memory_space=pltpu.VMEM),
+        functools.partial(block_kernel, n, heads, groups, inner_here * heads, features),
+        out_shape=[
+            jax.ShapeDtypeStruct((length, share), bf16),
+            jax.ShapeDtypeStruct(member.shape, f32),
+        ],
+        in_specs=[pl.BlockSpec(memory_space=pltpu.VMEM)] * (len(operands) + 1)
+        + [pl.BlockSpec(memory_space=pl.ANY)] * 2,
+        out_specs=[pl.BlockSpec(memory_space=pltpu.VMEM)] * 2,
         scratch_shapes=[
-            pltpu.VMEM((n, rows, deep), jnp.bfloat16),
-            pltpu.VMEM((deep, width), jnp.bfloat16),
-            pltpu.VMEM((n, 8, rows), jnp.int32),
-            pltpu.VMEM((n, 8, rows), jnp.float32),
-            pltpu.VMEM((peers, 8, TILE), jnp.float32),
-            pltpu.VMEM((peers,) + member.shape, jnp.float32),
-            dma,
-            dma((2, n, heads)),
-            dma((2, n, heads)),
+            vmem((inner_here, features), bf16),
+            vmem((features, width), bf16),
+            vmem((n, length, features), bf16),
+            vmem((n, 8, length), jnp.int32),
+            vmem((n, 8, length), f32),
+            vmem((peers, 8, TILE), f32),
+            vmem((peers,) + member.shape, f32),
+            vmem((HALO, inner_here), bf16),
+            vmem((HALO, 2 * STATE), bf16),
+            vmem((length + HALO, TILE), f32),
+            vmem((KERNEL - 1, length, TILE), f32),
+            vmem((length, inner_here), bf16),
+            vmem((length, 2 * STATE), bf16),
+            vmem((length, length), f32),
+            vmem((chunks, TILE, STATE), f32),
+            vmem((chunks, TILE, STATE), f32),
+            vmem((length, inner_here), f32),
+            vmem((length, TILE), f32),
+            vmem((2, heads, 8, length), f32),
+            vmem((length, inner_here), bf16),
+            vmem((4, length, share), f32),
+            vmem((3, length, share), f32),
+            vmem((length, share), bf16),
+            dma((2,)),
+            dma((2,)),
+            dma((2,)),
+            dma((n, PARTS)),
+            dma((n, PARTS)),
+            dma((n, PARTS, groups)),
+            dma((groups, n, PARTS)),
+            dma((chunks,)),
+            dma((chunks,)),
+            dma((2, heads)),
+            dma((2, heads)),
+            dma((3,)),
+            dma((3,)),
+            dma((4, n)),
+            dma((n,)),
             dma((n, heads)),
             dma((n,)),
             dma((n,)),
@@ -518,12 +846,101 @@
             dma((peers,)),
         ],
         compiler_params=pltpu.CompilerParams(
-            collective_id=0, has_side_effects=True, vmem_limit_bytes=60 * 2**20
+            collective_id=0, has_side_effects=True, vmem_limit_bytes=63 * 2**20
         ),
         cost_estimate=pl.CostEstimate(
-            flops=flops, bytes_accessed=deep * width * 2, transcendentals=n * rows * width
+            flops=2 * n * length * features * width, bytes_accessed=4 * 10**7, transcendentals=10**7
         ),
-    )(hidden_part, targets_row, member, weight)
+    )(*operands, member, *whole)
+
+
+def width_of(columns):
+    devices = lax.axis_size("seq")
+    return -(-columns // (devices * TILE)) * TILE
+
+
+def fused_fits(residual, x_in, lm_weight):
+    length, inner_here = x_in.shape
+    depth, columns = lm_weight.shape
+    sizes = [lax.axis_size(axis) for axis in ("seq", "head", "groups")]
+    return fits(
+        length, inner_here, residual.shape[1], depth, columns, width_of(columns), *sizes
+    )
+
+
+def fused(
+    residual,
+    x_in,
+    bc_in,
+    z_in,
+    dt_raw,
+    dt_bias,
+    decay_rate,
+    d_skip,
+    conv_x_weight,
+    conv_x_bias,
+    conv_bc_weight,
+    conv_bc_bias,
+    norm_gain,
+    out_weight,
+    final_gain,
+    lm_weight,
+    targets,
+    doc_lengths,
+):
+    length, _ = x_in.shape
+    heads_here = dt_raw.shape[0]
+    share = residual.shape[1]
+    head_rank = lax.axis_index("head")
+    offset_here = lax.axis_index("seq") * length
+    positions = offset_here + jnp.arange(length, dtype=jnp.int32)
+    doc_ids = document_of(positions, doc_lengths)
+    before = document_of(jnp.reshape(offset_here - 1, (1,)), doc_lengths)[0]
+    steps = jax.nn.softplus(dt_raw + dt_bias[:, None])
+    climb = jnp.cumsum(steps * decay_rate[:, None], axis=1)
+    last = (doc_ids == doc_ids[length - 1]).astype(jnp.float32)
+    tail = jnp.exp(climb - climb[:, length - 1 :]) * last[None, :] * steps
+    couples = heads_here // 2
+    rows = jnp.concatenate(
+        [climb.reshape(couples, 2, length), steps.reshape(couples, 2, length)], axis=1
+    )
+    cols = jnp.concatenate(
+        [climb.reshape(couples, 2, length), tail.reshape(couples, 2, length)], axis=1
+    ).transpose(0, 2, 1)
+    flags = [document_of(positions - lag, doc_lengths) == doc_ids for lag in range(KERNEL)]
+    flags += [doc_ids == before, doc_ids, doc_ids, doc_ids]
+    same = jnp.stack([flag.astype(jnp.float32) for flag in flags], axis=1)
+    doc_row = jnp.broadcast_to(doc_ids.astype(jnp.float32)[None, :], (8, length))
+    documents = -(-doc_lengths.shape[0] // 8) * 8
+    own_ids = lax.dynamic_slice_in_dim(doc_ids, head_rank * TILE, TILE, 0)
+    member = (own_ids[None, :] == jnp.arange(documents, dtype=jnp.int32)[:, None]).astype(
+        jnp.float32
+    )
+    final = lax.dynamic_slice_in_dim(final_gain, head_rank * share, share, 0)
+    operands = [
+        x_in,
+        z_in,
+        bc_in,
+        conv_x_weight.astype(jnp.float32),
+        conv_x_bias.astype(jnp.float32)[None, :],
+        conv_bc_weight.astype(jnp.float32),
+        conv_bc_bias.astype(jnp.float32)[None, :],
+        cols,
+        rows,
+        same,
+        doc_row,
+        jnp.repeat(d_skip, HEAD_SIZE)[None, :],
+        norm_gain.astype(jnp.float32)[None, :],
+        residual,
+        final.astype(jnp.float32)[None, :],
+        jnp.broadcast_to(targets[None, :], (8, length)),
+    ]
+    sizes = [lax.axis_size(axis) for axis in ("seq", "head", "groups")]
+    block_out, sums = block_stage(
+        operands, (out_weight, lm_weight), member, width_of(lm_weight.shape[1]), *sizes
+    )
+    sums = sums[: doc_lengths.shape[0], 0]
+    return (block_out, sums / doc_lengths.astype(jnp.float32))
 
 
 def local(
@@ -546,6 +963,27 @@
     targets,
     doc_lengths,
 ):
+    if fused_fits(residual, x_in, lm_weight):
+        return fused(
+            residual,
+            x_in,
+            bc_in,
+            z_in,
+            dt_raw,
+            dt_bias,
+            decay_rate,
+            d_skip,
+            conv_x_weight,
+            conv_x_bias,
+            conv_bc_weight,
+            conv_bc_bias,
+            norm_gain,
+            out_weight,
+            final_gain,
+            lm_weight,
+            targets,
+            doc_lengths,
+        )
     length = x_in.shape[0]
     inner_here = x_in.shape[1]
     heads_here = dt_raw.shape[0]
@@ -572,11 +1010,8 @@
         )
         for by in range(1, devices)
     ]
-    heads = lax.axis_size("head")
-    room = 2 * (devices * length * D + D * width) < 40 * 2**20
-    fused = room and heads == 4 and length == heads * TILE and share_of(residual) and devices > 1
     aims = [targets]
-    for by in range(1, 1 if fused else devices):
+    for by in range(1, devices):
         aims.append(rotated(targets, "seq", by))
     margin = KERNEL - 1
     rims = shifted(
@@ -672,21 +1107,6 @@
             vocab_weight = lax.dynamic_update_slice_in_dim(
                 vocab_weight, bands[by - 1][hop], start, 0
             )
-    if fused:
-        documents = -(-doc_lengths.shape[0] // 8) * 8
-        own_ids = lax.dynamic_slice_in_dim(doc_ids, head_rank * TILE, TILE, 0)
-        member = (own_ids[None, :] == jnp.arange(documents, dtype=jnp.int32)[:, None]).astype(
-            jnp.float32
-        )
-
-        def first_of(z, h, wide):
-            start = jnp.minimum(z * wide, columns_here - wide)
-            return z * wide - start, h * columns_here + start
-
-        row = jnp.broadcast_to(targets[None, :], (8, length))
-        sums = loss_stage(hidden_part, row, member, vocab_weight, devices, heads, first_of)
-        sums = sums[: doc_lengths.shape[0], 0]
-        return (block_out, sums / doc_lengths.astype(jnp.float32))
     column = jnp.arange(width, dtype=jnp.int32)
     first = head_rank * columns_here + window(seq_rank)
     live = column + window(seq_rank) >= seq_rank * width

time: 361 us -> 299 us (0.83)
  Pallas kernels: 125 us -> 273 us
  waiting for transfers between devices: 107 us -> 0 us
  starting transfers between devices: 43.7 us -> 0 us
  local copies, waits for them, and re-layouts: 42 us -> 13.5 us
  matrix products: 14.3 us -> 0 us
  blocking collectives: 11.5 us -> 0 us
  other arithmetic: 15.2 us -> 11.5 us
    pallas_call x3 -> x1, Pallas kernels: 125 us -> 273 us  [block_stage(): pl.pallas_call(functools.partial(block_kernel, n, heads, groups, inner_he...]
    ppermute x12 -> x0, waiting for transfers between devices: 107 us -> none  [the longest x7 88.9 us: rotated(): lax.ppermute(array, axis, [(i, (i + by) % length) for i in range(length)])]
    ppermute x12 -> x0, starting transfers between devices: 43.7 us -> none  [the longest x7 25.3 us: rotated(): lax.ppermute(array, axis, [(i, (i + by) % length) for i in range(length)])]
    dynamic_update_slice x7 -> x0, local copies, waits for them, and re-layouts: 15.4 us -> none  [the longest x6 11.5 us: local(): lax.dynamic_update_slice_in_dim(vocab_weight, bands[by - 1][hop], start, 0)]
    dot_general x6 -> x0, matrix products: 14.3 us -> none  [the longest x1 5.46 us: scattered_product(): other = jnp.dot(normed, theirs, preferred_element_type=jnp.float32)]
    psum x2 -> x0, blocking collectives: 11.5 us -> none  [the longest x1 5.84 us: local(): square_sum = lax.psum(jnp.sum(gated * gated, axis=1), 'head')]
    dynamic_slice x3 -> x1, local copies, waits for them, and re-layouts: 11.5 us -> 0.07 us  [fused(): own_ids = lax.dynamic_slice_in_dim(doc_ids, head_rank * TILE, TILE, 0)]
  transfers between devices with their start and end apart: 12 -> 0, of which waited for: 7 -> 0; matrix products, arithmetic and copies ran while one was open for 15% -> 0% of each run, Pallas kernels for 3% -> 0%
where the time goes in v1:
time: 299 us
  Pallas kernels  273 us (91%)
  local copies, waits for them, and re-layouts  13.5 us (5%)
  other arithmetic  11.5 us (4%)
    pallas_call x1, Pallas kernels, block_stage(): pl.pallas_call(functools.partial(block_kernel, n, heads, groups, inner_he...  273 us

profile of v1, /device:TPU:0, one launch (start us, length us, event | category | flops | bytes accessed | tf_op | source)
XLA Modules:
  0.0 299.0 jit_solution(12617878611104004287)
XLA Ops:
  0.6 0.8 reduce-window.21
  1.5 1.3 fusion.8
  3.4 1.2 broadcast_in_dim.63
  4.6 0.8 dynamic-slice_convert_fusion
  5.3 0.6 reshape.193.final_ref
  5.9 1.3 convert_element_type.116.bc_taps_ref
  7.2 0.1 convert_reduce_fusion
  7.3 0.6 slice.18
  7.9 0.1 dynamic_slice.7
  8.0 0.6 compare_convert_fusion
  8.6 0.6 fusion.1.member_ref
  9.2 1.3 reshape.186.bias_ref
  10.5 1.3 reshape.192.gain_ref
  11.8 0.7 broadcast_in_dim.27
  12.6 0.7 broadcast_in_dim_reshape.4.skip_ref
  13.2 0.6 broadcast_in_dim.26.doc_ref
  13.8 1.3 broadcast_in_dim.61.tgt_ref
  15.1 1.3 convert_element_type.115.taps_ref
  16.4 0.9 broadcast_multiply_fusion
  17.4 1.2 reduce-window.19
  18.5 0.2 slice_reduce_fusion
  18.7 0.1 broadcast_add_fusion
  18.9 0.2 slice_reduce_fusion.1
  19.1 0.1 multiply_multiply_fusion
  19.3 0.7 pad_maximum_fusion
  20.0 0.8 copy.43.same_ref
  20.8 2.3 copy.42.cols_ref
  23.1 272.6 %shard_map.185 = (bf16[512,640]{1,0:T(8,128)(2,1)}, f32[8,128]{1,0:T(8,128)}) custom-call(bf16[512,1280]{1,0:T(8,128)(2,1)} %x_ref.1, bf16[512,1280]{1,0:T(8,128)(2,1)} %z_ref.1, bf16[512,256]{1,0:T(8,128)(2,1)} %bc_ref.1, f32[4,1280]{1,0:T(4,128)} %convert_element_type.115.taps_ref, f32[1,1280]{1,0:T(1,128)} %reshape.186.bias_ref, ...), custom_call_target="tpu_custom_call" | custom-call | flops 17448304640 | bytes 40000000 | tf_op jit(solution)/shard_map/pallas_call | solution.py:792
  295.7 0.8 slice_reduce_fusion.2
  296.5 0.0 copy-done
  296.5 0.5 convert_divide_fusion
  297.0 2.0 copy.46
  (16 shorter events, 0.2 us)
Async XLA Ops:
  23.1 273.4 %copy-start = (s32[4]{0:T(128)S(1)}, s32[4]{0:T(128)}, u32[]{:S(2)}) copy-start(s32[4]{0:T(128)} %param.35) | copy-start | bytes 52
